TPU v7x, 32 devices: a whole 2x2x4 slice. The times are simulated.
32 devices in a mesh: dp: 8 (over z, x), mp: 4 (over y, core).
Axes of the slice: x: 2, y: 2, z: 4, core: 2. Of those that a mesh axis runs over, the one named last changes fastest.
Arguments:
- inputs: bfloat16 [6144, 4608], P('dp'), may hold values from -8 to 8
- key_cotangent: bfloat16 [6144, 2048], P('dp', 'mp'), may hold values from -8 to 8
- master: float32 [4608, 2048], P('dp', 'mp'), may hold values from -0.09375 to 0.09375
- first_codes: int32 [4608, 2048], P('dp', 'mp'), may hold values from -127 to 127
- second_codes: int32 [4608, 2048], P('dp', 'mp'), may hold values from 1 to 255
- first_scale: float32 [1152, 4], P('dp', 'mp'), may hold values from 0.05 to 0.5
- second_scale: float32 [1152, 4], P('dp', 'mp'), may hold values from 0.02 to 0.2
Outputs:
- weight: bfloat16 [4608, 2048], P(None, 'mp')
- new_master: float32 [4608, 2048], P('dp', 'mp')
- first_unit: float32 [4608, 2048], P('dp', 'mp')
- second_unit: float32 [4608, 2048], P('dp', 'mp')
- first_top: float32 [1152, 4], P('dp', 'mp')
- second_top: float32 [1152, 4], P('dp', 'mp')
All inputs are finite; a program needn't handle non-finite values. Where the computation divides by a largest or mean magnitude, that divisor is 1e-20 or more.
Results may differ from a plain program's by a relative error of at most 0.0004.
Values may be sent and summed in bfloat16 or wider, within the bound.
A program may use at most 128 MiB of HBM per device.

v0:
```python
import math

import jax
import jax.numpy as jnp
from jax import lax
from jax.sharding import PartitionSpec as P

D = 4608
KV = 2048
QROWS = 4
QCOLS = 512
STEP = 10


beta_one = 0.9
beta_two = 0.95
learn_rate = 0.002
weight_decay = 0.1
epsilon = 1e-08
clip_rms = 0.25


def blocks(array):
    return array.reshape(array.shape[0] // QROWS, QROWS, array.shape[1] // QCOLS, QCOLS)


def adam_step(gradient, norm_sq, master, first_codes, second_codes, first_scale, second_scale):
    factor = jnp.minimum(1.0, clip_rms * math.sqrt(D * KV) / (jnp.sqrt(norm_sq) + 1e-06))
    clipped = blocks(gradient * factor)
    first_old = blocks(first_codes.astype(jnp.float32)) / 127.0 * first_scale[:, None, :, None]
    second_old = blocks(second_codes.astype(jnp.float32)) / 255.0 * second_scale[:, None, :, None]
    first_new = beta_one * first_old + (1.0 - beta_one) * clipped
    second_new = beta_two * second_old + (1.0 - beta_two) * clipped * clipped
    first_hat = first_new / (1.0 - beta_one**STEP)
    second_hat = second_new / (1.0 - beta_two**STEP)
    step_dir = (first_hat / (jnp.sqrt(second_hat) + epsilon)).reshape(master.shape)
    new_master = master - learn_rate * (step_dir + weight_decay * master)
    first_top = jnp.max(jnp.abs(first_new), axis=(1, 3)) + 1e-06
    second_top = jnp.max(second_new, axis=(1, 3)) + 1e-06
    first_unit = (first_new / first_top[:, None, :, None]).reshape(master.shape)
    second_unit = (second_new / second_top[:, None, :, None]).reshape(master.shape)
    return (new_master, first_unit, second_unit, first_top, second_top)


def shards(inputs, key_cotangent, master, first_codes, second_codes, first_scale, second_scale):
    contract = (((0,), (0,)), ((), ()))
    full_term = lax.dot_general(inputs, key_cotangent, contract, preferred_element_type=jnp.float32)
    gradient = lax.psum_scatter(full_term, "dp", scatter_dimension=0, tiled=True)
    norm_sq = lax.psum(jnp.sum(gradient * gradient), ("dp", "mp"))
    new_master, first_unit, second_unit, first_top, second_top = adam_step(
        gradient, norm_sq, master, first_codes, second_codes, first_scale, second_scale
    )
    weight = lax.all_gather(new_master.astype(jnp.bfloat16), "dp", axis=0, tiled=True)
    return (weight, new_master, first_unit, second_unit, first_top, second_top)


def solution(mesh):
    return jax.shard_map(
        shards,
        mesh=mesh,
        in_specs=(
            P("dp", None),
            P("dp", "mp"),
            P("dp", "mp"),
            P("dp", "mp"),
            P("dp", "mp"),
            P("dp", "mp"),
            P("dp", "mp"),
        ),
        out_specs=(
            P(None, "mp"),
            P("dp", "mp"),
            P("dp", "mp"),
            P("dp", "mp"),
            P("dp", "mp"),
            P("dp", "mp"),
        ),
        check_vma=False,
    )
```

profile of v0, /device:TPU:0, one launch (start us, length us, event | category | flops | bytes accessed | tf_op | source)
XLA Modules:
  0.0 325.2 jit_solution(8230839865846537582)
XLA Ops:
  7.2 0.0 copy-start
  7.2 0.0 reduce-scatter.2.cloned.1.call-start
  7.2 1.1 copy-done
  8.3 9.4 %fusion.4 = f32[4608,512]{1,0:T(8,128)} fusion(bf16[768,4608]{1,0:T(8,128)(2,1)} %param.7, bf16[768,512]{1,0:T(8,128)(2,1)S(1)} %copy-done), kind=kOutput, calls=%fused_computation.14 | convolution fusion | flops 3623878656 | bytes 17301504 | tf_op jit(solution)/shard_map/dot_general | solution.py:47
  17.7 0.0 copy-start.4
  17.7 0.0 copy-start.5
  17.7 0.0 reduce-scatter.2.cloned.1.call-update
  17.8 0.0 all-gather.2.cloned.1.call-start
  17.8 0.6 copy-done.4
  18.4 0.1 mul.148
  18.5 0.1 mul.149
  18.6 0.0 copy-done.5
  18.6 164.1 %reduce-scatter.2.cloned.1.call-done = f32[576,512]{1,0:T(8,128)} async-done(((f32[4608,512]{1,0:T(8,128)}), f32[576,512]{1,0:T(8,128)}) %reduce-scatter.2.cloned.1.call-update) | async-done | bytes 1179664 | tf_op jit(solution)/shard_map/reduce_scatter | solution.py:48
  182.8 0.0 copy-start.1
  182.8 2.3 multiply_reduce_fusion
  185.0 0.1 mul.134
  185.1 0.1 mul.135
  185.2 39.5 %psum.7 = f32[]{:T(128)} all-reduce(f32[]{:T(128)} %multiply_reduce_fusion), channel_id=1, replica_groups=mesh['dp'=8,'mp'=4] {'dp','mp'}, use_global_device_ids=true, to_apply=%region_2.0 | all-reduce | flops 1 | bytes 8 | tf_op jit(solution)/shard_map/psum | solution.py:49
  225.5 0.0 copy-done.1
  225.5 3.3 %abs_reduce_fusion = (f32[576]{0:T(1024)S(1)}, f32[576,512]{1,0:T(8,128)S(1)}, f32[576]{0:T(1024)S(1)}, f32[576,512]{1,0:T(8,128)}) fusion(f32[576,512]{1,0:T(8,128)S(1)} %copy-done.1, f32[]{:T(128)S(6)} %min_shard_map.3, f32[576]{0:T(1024)S(1)} %mul.135, s32[576,512]{1,0:T(8,128)} %param.10, f32[576]{0:T(1024)S(1)} %mul.149, s32[576,512]{1,0:T(8,128)} %param.11), kind=kLoop, calls=%fused_computation.2 | loop fusion | flops 4422528 | bytes 5907460 | tf_op jit(solution)/shard_map/reduce_max | solution.py:38
  228.9 0.1 reduce_max.24
  229.0 0.1 reduce_max.25
  229.1 0.0 copy-start.2
  229.1 0.1 div.61
  229.2 0.1 div.62
  229.3 0.1 reduce_max.36
  229.4 0.1 reduce_max.37
  229.5 0.0 copy-start.3
  229.6 0.1 div.65
  229.6 0.1 div.66
  229.7 4.4 %fusion.3 = (bf16[576,512]{1,0:T(8,128)(2,1)}, f32[576,512]{1,0:T(8,128)}, f32[576,512]{1,0:T(8,128)}, f32[576,512]{1,0:T(8,128)}) fusion(f32[576,512]{1,0:T(8,128)} %param.9, f32[576,512]{1,0:T(8,128)} %get-tuple-element.15, f32[576,512]{1,0:T(8,128)S(1)} %get-tuple-element.9, f32[576]{0:T(1024)S(1)} %div.66, f32[576]{0:T(1024)S(1)} %div.62), kind=kLoop, calls=%fused_computation.13 | loop fusion | flops 3244032 | bytes 7672320 | tf_op jit(solution)/shard_map/convert_element_type | solution.py:53
  234.1 0.0 copy-done.2
  234.1 0.0 copy-done.3
  234.1 0.0 all-gather.2.cloned.1.call-update
  234.1 79.4 %all-gather.2.cloned.1.call-done = bf16[4608,512]{1,0:T(8,128)(2,1)} async-done(((bf16[576,512]{1,0:T(8,128)(2,1)}), bf16[4608,512]{1,0:T(8,128)(2,1)}) %all-gather.2.cloned.1.call-update) | async-done | bytes 4718608 | tf_op jit(solution)/shard_map/all_gather | solution.py:53
  313.6 4.8 %copy.14 = bf16[4608,512]{1,0:T(8,128)(2,1)} copy(bf16[4608,512]{1,0:T(8,128)(2,1)} %all-gather.2.cloned.1.call-done) | data formatting | bytes 9437184
  (4 shorter events, 0.0 us)
Async XLA Ops:
  7.2 1.1 copy-start
  7.2 175.6 %reduce-scatter.2.cloned.1.call-start = ((), (), s32[]{:S(2)}) async-start(), calls=%async_computation.1 | async-start | bytes 10616832 | tf_op jit(solution)/shard_map/reduce_scatter | solution.py:48
  17.7 0.7 copy-start.4
  17.7 0.9 copy-start.5
  17.8 295.8 %all-gather.2.cloned.1.call-start = ((), (), s32[]{:S(2)}) async-start(), calls=%async_computation.2 | async-start | bytes 5308416 | tf_op jit(solution)/shard_map/all_gather | solution.py:53
  182.8 42.8 %copy-start.1 = (f32[576,512]{1,0:T(8,128)S(1)}, f32[576,512]{1,0:T(8,128)}, u32[]{:S(2)}) copy-start(f32[576,512]{1,0:T(8,128)} %reduce-scatter.2.cloned.1.call-done) | copy-start | bytes 3538948
  229.1 5.0 %copy-start.2 = (f32[144]{0:T(256)}, f32[144]{0:T(256)S(1)}, u32[]{:S(2)}) copy-start(f32[144]{0:T(256)S(1)} %broadcast_add_fusion.1) | copy-start | bytes 1732
  229.5 4.6 %copy-start.3 = (f32[144]{0:T(256)}, f32[144]{0:T(256)S(1)}, u32[]{:S(2)}) copy-start(f32[144]{0:T(256)S(1)} %broadcast_add_fusion) | copy-start | bytes 1732
Sparse Core Ops, SparseCore 0:
  17.9 164.8 reduce-scatter.1
  234.2 79.2 all-gather.1
where the time goes:
time: 326 us; the launch traced here: 325 us
  waiting for transfers between devices  244 us (75%)
  blocking collectives  39.5 us (12%)
  between operations  14.9 us (5%)
  other arithmetic  10.2 us (3%)
  matrix products  9.42 us (3%)
  local copies, waits for them, and re-layouts  7.47 us (2%)
    reduce_scatter x1, waiting for transfers between devices, shards(): lax.psum_scatter(full_term, 'dp', scatter_dimension=0, tiled=True)  164 us
    all_gather x1, waiting for transfers between devices, shards(): lax.all_gather(new_master.astype(jnp.bfloat16), 'dp', axis=0, tiled=True)  79.4 us
    psum x1, blocking collectives, shards(): norm_sq = lax.psum(jnp.sum(gradient * gradient), ('dp', 'mp'))  39.5 us
    dot_general x1, matrix products, shards(): lax.dot_general(inputs, key_cotangent, contract, preferred_element_type=j...  9.42 us
    unnamed x13, local copies, waits for them, and re-layouts  6.53 us
  transfers between devices with their start and end apart: 2, of which 2 were waited for; matrix products, arithmetic and copies ran while one was open for 0% of the time, Pallas kernels for 0%

commit v1 on v0

v1 whole, which is shorter than its diff:
```python
import functools
import math

import jax
import jax.numpy as jnp
from jax import lax
from jax.experimental import pallas as pl
from jax.experimental.pallas import tpu as pltpu
from jax.sharding import PartitionSpec as P

MESH = pl.DeviceIdType.MESH
QROWS = 4
STEP = 10
LANES = 128

beta_one = 0.9
beta_two = 0.95
learn_rate = 0.002
weight_decay = 0.1
epsilon = 1e-08
clip_rms = 0.25
CODE_MAX = 32767.0


def kernel(
    n,
    m,
    limit,
    x_hbm,
    cot_hbm,
    master_hbm,
    fc_hbm,
    sc_hbm,
    fscale_ref,
    sscale_ref,
    w_hbm,
    nm_hbm,
    fu_hbm,
    su_hbm,
    ftop_ref,
    stop_ref,
    x_v,
    cot_v,
    part,
    xs,
    xs_s,
    xr,
    xr_s,
    zs,
    zs_s,
    zr,
    zr_s,
    master,
    fc,
    sc,
    fn,
    sn,
    nm_v,
    fu_v,
    su_v,
    row1,
    row2,
    wbuf,
    nd_out,
    nd_in,
    nm_out,
    nm_in,
    in_sem,
    par_sem,
    xs_send,
    xs_recv,
    xss_send,
    xss_recv,
    zs_send,
    zs_recv,
    zss_send,
    zss_recv,
    nd_send,
    nd_recv,
    nmx_send,
    nmx_recv,
    wx_send,
    wx_recv,
    wz_send,
    wz_recv,
    wout_sem,
    out_sem,
):
    B = 2
    A = n // B
    rows, width = master.shape
    cols_total = x_v.shape[1]
    R = 96 if rows % 96 == 0 else rows
    NR = rows // R
    Q = rows // QROWS
    REP = width // LANES

    me = lax.axis_index("dp")
    my = lax.axis_index("mp")
    a = me // B
    b = me % B
    mate = a * B + (1 - b)

    hi = A - 1 - a
    lo = a
    up_longer = jnp.where(hi >= lo, 1, -1)
    short = jnp.minimum(hi, lo)
    long = jnp.maximum(hi, lo)

    def order(i):
        j = i - (long - short)
        d_far = long - i
        jj = jnp.maximum(j, 0)
        d_near = short - jj // 2
        sgn = jnp.where(jj % 2 == 0, up_longer, -up_longer)
        return jnp.where(j < 0, a + up_longer * d_far, a + sgn * d_near)

    per_chunk = (B * rows) % 384 == 0
    csize = B * rows

    def in_copy(c):
        if per_chunk:
            sl = pl.ds(pl.multiple_of(c * csize, LANES), csize)
            return pltpu.make_async_copy(x_hbm.at[:, sl], x_v.at[:, sl], in_sem.at[c])
        return pltpu.make_async_copy(x_hbm, x_v, in_sem.at[0])

    cot_copy = pltpu.make_async_copy(cot_hbm, cot_v, par_sem.at[0])
    par_copies = [
        pltpu.make_async_copy(src, dst, par_sem.at[k + 1])
        for k, (src, dst) in enumerate(((master_hbm, master), (fc_hbm, fc), (sc_hbm, sc)))
    ]
    cot_copy.start()
    if per_chunk:

        @pl.loop(0, A)
        def _(i):
            in_copy(order(i)).start()
    else:
        in_copy(0).start()
    for cp in par_copies:
        cp.start()

    barrier = pltpu.get_barrier_semaphore()

    @pl.loop(1, n)
    def _(k):
        pl.semaphore_signal(barrier, inc=1, device_id={"dp": (me + k) % n}, device_id_type=MESH)

    @pl.loop(1, m)
    def _(k):
        pl.semaphore_signal(barrier, inc=1, device_id={"mp": (my + k) % m}, device_id_type=MESH)

    def multiply(first, count):
        @pl.loop(0, count)
        def _(k):
            at = pl.ds(pl.multiple_of(first + k * 384, LANES), 384)
            part[at, :] = lax.dot_general(
                x_v[:, at], cot_v[...], (((0,), (0,)), ((), ())), preferred_element_type=jnp.float32
            )

    def at_rows(block, r):
        return pl.ds(pl.multiple_of(block * rows + r * R, 8), R)

    def chunk_rows(r):
        return pl.ds(pl.multiple_of(r * R, 8), R)

    def fold(v):
        return v.reshape(R // 8, 8, width)

    def encode(block, dst, dst_s, top):
        top = jnp.maximum(top, 1e-30)
        dst_s[...] = top * (1.0 / CODE_MAX)
        inv = (CODE_MAX / top)[None]

        @pl.loop(0, NR)
        def _(r):
            v = jnp.round(fold(part[at_rows(block, r), :]) * inv).reshape(R, width)
            dst[chunk_rows(r), :] = v.astype(jnp.int32).astype(jnp.int16)

    def top_of(block):
        def body(r, t):
            return jnp.maximum(t, jnp.max(jnp.abs(fold(part[at_rows(block, r), :])), axis=0))

        return lax.fori_loop(0, NR, body, jnp.zeros((8, width), jnp.float32))

    def add(block, src, src_s):
        s = src_s[...][None]

        @pl.loop(0, NR)
        def _(r):
            v = fold(src[chunk_rows(r), :].astype(jnp.int32).astype(jnp.float32)) * s
            part[at_rows(block, r), :] = part[at_rows(block, r), :] + v.reshape(R, width)

    def pair_copies(c):
        to = {"dp": mate}
        return (
            pltpu.make_async_remote_copy(
                xs.at[c], xr.at[c], xs_send.at[c], xs_recv.at[c], device_id=to, device_id_type=MESH
            ),
            pltpu.make_async_remote_copy(
                xs_s.at[c], xr_s.at[c], xss_send.at[c], xss_recv.at[c], device_id=to, device_id_type=MESH
            ),
        )

    def line_copies(c, slot, to):
        to = {"dp": to}
        return (
            pltpu.make_async_remote_copy(
                zs.at[c], zr.at[slot], zs_send.at[c], zs_recv.at[slot], device_id=to, device_id_type=MESH
            ),
            pltpu.make_async_remote_copy(
                zs_s.at[c], zr_s.at[slot], zss_send.at[c], zss_recv.at[slot], device_id=to, device_id_type=MESH
            ),
        )

    cot_copy.wait()
    if not per_chunk:
        in_copy(0).wait()
        multiply(0, cols_total // 384)

    @pl.loop(0, A)
    def _(i):
        c = order(i)
        if per_chunk:
            in_copy(c).wait()
            multiply(c * csize, csize // 384)
        block = c * B + (1 - b)
        encode(block, xs.at[c], xs_s.at[c], top_of(block))

        @pl.when(i == 0)
        def _():
            pl.semaphore_wait(barrier, n - 1 + m - 1)

        for cp in pair_copies(c):
            cp.start()

    def receive(c, slot):
        for cp in line_copies(c, slot, me):
            cp.wait_recv()
        add(c * B + b, zr.at[slot], zr_s.at[slot])

    def forward(c, slot, to):
        block = c * B + b
        encode(block, zs.at[c], zs_s.at[c], top_of(block))
        for cp in line_copies(c, slot, to):
            cp.start()

    @pl.loop(0, A)
    def _(i):
        c = order(i)
        for cp in pair_copies(c):
            cp.wait_recv()
        add(c * B + b, xr.at[c], xr_s.at[c])

        @pl.when((c >= a) & (a > 0))
        def _():
            receive(c, c)

        @pl.when((c <= a) & (a < A - 1))
        def _():
            receive(c, A + c)

        @pl.when(c > a)
        def _():
            forward(c, c, me + B)

        @pl.when(c < a)
        def _():
            forward(c, A + c, me - B)

    def square(r, t):
        g = fold(part[at_rows(me, r), :])
        return t + jnp.sum(g * g, axis=0)

    squares = lax.fori_loop(0, NR, square, jnp.zeros((8, width), jnp.float32))
    mine = squares[:, :LANES]
    for k in range(1, REP):
        mine = mine + squares[:, k * LANES : (k + 1) * LANES]

    def exchange(axis, size, own, value, out, inbox, send, recv):
        out[...] = value
        inbox[own] = value

        def copy(k, slot):
            return pltpu.make_async_remote_copy(
                out,
                inbox.at[slot],
                send.at[k],
                recv.at[slot],
                device_id={axis: (own + k) % size},
                device_id_type=MESH,
            )

        @pl.loop(1, size)
        def _(k):
            copy(k, own).start()

        @pl.loop(1, size)
        def _(k):
            copy(k, (own + k) % size).wait_recv()

        @pl.loop(1, size)
        def _(k):
            copy(k, own).wait_send()

        return jnp.sum(inbox[...], axis=0)

    over_dp = exchange("dp", n, me, mine, nd_out, nd_in, nd_send, nd_recv)
    over_all = exchange("mp", m, my, over_dp, nm_out, nm_in, nmx_send, nmx_recv)
    norm_sq = jnp.sum(jnp.sum(over_all, axis=0, keepdims=True), axis=1, keepdims=True)
    factor = jnp.minimum(1.0, limit / (jnp.sqrt(norm_sq) + 1e-06))

    for cp in par_copies:
        cp.wait()
    for j in range(QROWS):
        every = pl.ds(j, Q, stride=QROWS)
        row1[every, :] = jnp.broadcast_to(fscale_ref[...] * (1.0 / 127.0), (Q, LANES))
        row2[every, :] = jnp.broadcast_to(sscale_ref[...] * (1.0 / 255.0), (Q, LANES))

    def wide(v):
        return jnp.concatenate([v] * REP, axis=1)

    @pl.loop(0, NR)
    def _(r):
        at = chunk_rows(r)
        clipped = part[at_rows(me, r), :] * factor
        first_new = beta_one * (fc[at, :].astype(jnp.float32) * wide(row1[at, :])) + (1.0 - beta_one) * clipped
        second_new = (
            beta_two * (sc[at, :].astype(jnp.float32) * wide(row2[at, :])) + (1.0 - beta_two) * clipped * clipped
        )
        fn[at, :] = first_new
        sn[at, :] = second_new
        first_hat = first_new * (1.0 / (1.0 - beta_one**STEP))
        second_hat = second_new * (1.0 / (1.0 - beta_two**STEP))
        step_dir = first_hat / (jnp.sqrt(second_hat) + epsilon)
        old = master[at, :]
        new = old - learn_rate * (step_dir + weight_decay * old)
        nm_v[at, :] = new
        wbuf[me, at, :] = new.astype(jnp.bfloat16)

    def pair_weight(c, block):
        return pltpu.make_async_remote_copy(
            wbuf.at[block],
            wbuf.at[block],
            wx_send.at[c],
            wx_recv.at[c],
            device_id={"dp": mate},
            device_id_type=MESH,
        )

    def line_weight(c, way, to):
        block = c * B + b
        return pltpu.make_async_remote_copy(
            wbuf.at[block],
            wbuf.at[block],
            wz_send.at[way * A + c],
            wz_recv.at[c],
            device_id={"dp": to},
            device_id_type=MESH,
        )

    def weight_out(block):
        return pltpu.make_async_copy(wbuf.at[block], w_hbm.at[block], wout_sem.at[block])

    @pl.when(a < A - 1)
    def _():
        line_weight(a, 0, me + B).start()

    @pl.when(a > 0)
    def _():
        line_weight(a, 1, me - B).start()

    pair_weight(a, me).start()
    weight_out(me).start()
    nm_out_copy = pltpu.make_async_copy(nm_v, nm_hbm, out_sem.at[0])
    fu_out_copy = pltpu.make_async_copy(fu_v, fu_hbm, out_sem.at[1])
    su_out_copy = pltpu.make_async_copy(su_v, su_hbm, out_sem.at[2])
    nm_out_copy.start()

    @pl.loop(0, NR)
    def _(r):
        at = chunk_rows(r)
        row1[at, :] = jnp.broadcast_to(jnp.max(jnp.abs(fn[at, :]), axis=1, keepdims=True), (R, LANES))
        row2[at, :] = jnp.broadcast_to(jnp.max(sn[at, :], axis=1, keepdims=True), (R, LANES))

    for row, top_ref in ((row1, ftop_ref), (row2, stop_ref)):
        top = row[pl.ds(0, Q, stride=QROWS), :]
        for j in range(1, QROWS):
            top = jnp.maximum(top, row[pl.ds(j, Q, stride=QROWS), :])
        top = top + 1e-06
        top_ref[...] = top[:, :1]
        for j in range(QROWS):
            row[pl.ds(j, Q, stride=QROWS), :] = 1.0 / top

    @pl.loop(0, NR)
    def _(r):
        at = chunk_rows(r)
        fu_v[at, :] = fn[at, :] * wide(row1[at, :])
        su_v[at, :] = sn[at, :] * wide(row2[at, :])

    fu_out_copy.start()
    su_out_copy.start()

    @pl.loop(1, A)
    def _(d):
        @pl.when(a - d >= 0)
        def _():
            c = a - d
            line_weight(c, 0, me).wait_recv()

            @pl.when(a < A - 1)
            def _():
                line_weight(c, 0, me + B).start()

            pair_weight(c, c * B + b).start()
            weight_out(c * B + b).start()

        @pl.when(a + d < A)
        def _():
            c = a + d
            line_weight(c, 1, me).wait_recv()

            @pl.when(a > 0)
            def _():
                line_weight(c, 1, me - B).start()

            pair_weight(c, c * B + b).start()
            weight_out(c * B + b).start()

        @pl.when(d == 1)
        def _():
            pair_weight(a, mate).wait_recv()
            weight_out(mate).start()

    @pl.loop(1, A)
    def _(d):
        @pl.when(a - d >= 0)
        def _():
            c = a - d
            pair_weight(c, c * B + 1 - b).wait_recv()
            weight_out(c * B + 1 - b).start()

        @pl.when(a + d < A)
        def _():
            c = a + d
            pair_weight(c, c * B + 1 - b).wait_recv()
            weight_out(c * B + 1 - b).start()

    @pl.loop(0, A)
    def _(c):
        for cp in pair_copies(c):
            cp.wait_send()

        @pl.when(c != a)
        def _():
            for cp in line_copies(c, c, me):
                cp.wait_send()

        pair_weight(c, c * B + b).wait_send()

        @pl.when((c <= a) & (a < A - 1))
        def _():
            line_weight(c, 0, me).wait_send()

        @pl.when((c >= a) & (a > 0))
        def _():
            line_weight(c, 1, me).wait_send()

    @pl.loop(0, n)
    def _(k):
        weight_out(k).wait()

    nm_out_copy.wait()
    fu_out_copy.wait()
    su_out_copy.wait()


def shards(n, m, limit, inputs, key_cotangent, master, first_codes, second_codes, first_scale, second_scale):
    rows, width = master.shape
    tokens, cols = inputs.shape
    A = n // 2
    f32 = jnp.float32
    any_spec = pl.BlockSpec(memory_space=pl.ANY)
    vmem_spec = pl.BlockSpec(memory_space=pltpu.VMEM)
    dma = pltpu.SemaphoreType.DMA
    block = (rows, width)
    outs = pl.pallas_call(
        functools.partial(kernel, n, m, limit),
        out_shape=(
            jax.ShapeDtypeStruct((n, rows, width), jnp.bfloat16),
            jax.ShapeDtypeStruct(block, f32),
            jax.ShapeDtypeStruct(block, f32),
            jax.ShapeDtypeStruct(block, f32),
            jax.ShapeDtypeStruct(first_scale.shape, f32),
            jax.ShapeDtypeStruct(second_scale.shape, f32),
        ),
        in_specs=[any_spec] * 5 + [vmem_spec] * 2,
        out_specs=[any_spec] * 4 + [vmem_spec] * 2,
        scratch_shapes=[
            pltpu.VMEM((tokens, cols), jnp.bfloat16),
            pltpu.VMEM(key_cotangent.shape, jnp.bfloat16),
            pltpu.VMEM((cols, width), f32),
            pltpu.VMEM((A, rows, width), jnp.int16),
            pltpu.VMEM((A, 8, width), f32),
            pltpu.VMEM((A, rows, width), jnp.int16),
            pltpu.VMEM((A, 8, width), f32),
            pltpu.VMEM((A, rows, width), jnp.int16),
            pltpu.VMEM((A, 8, width), f32),
            pltpu.VMEM((2 * A, rows, width), jnp.int16),
            pltpu.VMEM((2 * A, 8, width), f32),
            pltpu.VMEM(block, f32),
            pltpu.VMEM(block, jnp.int32),
            pltpu.VMEM(block, jnp.int32),
            pltpu.VMEM(block, f32),
            pltpu.VMEM(block, f32),
            pltpu.VMEM(block, f32),
            pltpu.VMEM(block, f32),
            pltpu.VMEM(block, f32),
            pltpu.VMEM((rows, LANES), f32),
            pltpu.VMEM((rows, LANES), f32),
            pltpu.VMEM((n, rows, width), jnp.bfloat16),
            pltpu.VMEM((8, LANES), f32),
            pltpu.VMEM((n, 8, LANES), f32),
            pltpu.VMEM((8, LANES), f32),
            pltpu.VMEM((m, 8, LANES), f32),
            dma((A,)),
            dma((4,)),
            dma((A,)),
            dma((A,)),
            dma((A,)),
            dma((A,)),
            dma((A,)),
            dma((2 * A,)),
            dma((A,)),
            dma((2 * A,)),
            dma((n,)),
            dma((n,)),
            dma((m,)),
            dma((m,)),
            dma((A,)),
            dma((A,)),
            dma((2 * A,)),
            dma((A,)),
            dma((n,)),
            dma((3,)),
        ],
        compiler_params=pltpu.CompilerParams(
            collective_id=0, has_side_effects=True, vmem_limit_bytes=62 * 1024 * 1024
        ),
        name="step",
    )(inputs, key_cotangent, master, first_codes, second_codes, first_scale, second_scale)
    weight = outs[0].reshape(n * rows, width)
    return (weight, *outs[1:])


def solution(mesh):
    n, m = mesh.shape["dp"], mesh.shape["mp"]

    def run(inputs, key_cotangent, master, *rest):
        limit = clip_rms * math.sqrt(inputs.shape[1] * key_cotangent.shape[1])
        return jax.shard_map(
            functools.partial(shards, n, m, limit),
            mesh=mesh,
            in_specs=(
                P("dp", None),
                P("dp", "mp"),
                P("dp", "mp"),
                P("dp", "mp"),
                P("dp", "mp"),
                P("dp", "mp"),
                P("dp", "mp"),
            ),
            out_specs=(
                P(None, "mp"),
                P("dp", "mp"),
                P("dp", "mp"),
                P("dp", "mp"),
                P("dp", "mp"),
                P("dp", "mp"),
            ),
            check_vma=False,
        )(inputs, key_cotangent, master, *rest)

    return run
```

time: 326 us -> 147 us (0.45)
  waiting for transfers between devices: 244 us -> 0 us
  Pallas kernels: 0 us -> 131 us
  blocking collectives: 39.5 us -> 0 us
  between operations: 14.9 us -> 0.65 us
  other arithmetic: 10.2 us -> 0 us
  matrix products: 9.42 us -> 0 us
  local copies, waits for them, and re-layouts: 7.47 us -> 15.2 us
    reduce_scatter x1 -> x0, waiting for transfers between devices: 164 us -> none  [shards(): lax.psum_scatter(full_term, 'dp', scatter_dimension=0, tiled=True)]
    pallas_call x0 -> x1, Pallas kernels: none -> 131 us  [shards(): pl.pallas_call(functools.partial(kernel, n, m, limit), out_shape=(jax.Sha...]
    all_gather x1 -> x0, waiting for transfers between devices: 79.4 us -> none  [shards(): lax.all_gather(new_master.astype(jnp.bfloat16), 'dp', axis=0, tiled=True)]
    psum x1 -> x0, blocking collectives: 39.5 us -> none  [shards(): norm_sq = lax.psum(jnp.sum(gradient * gradient), ('dp', 'mp'))]
    dot_general x1 -> x0, matrix products: 9.42 us -> none  [shards(): lax.dot_general(inputs, key_cotangent, contract, preferred_element_type=j...]
    unnamed x13 -> x14, local copies, waits for them, and re-layouts: 6.53 us -> 15.2 us
    convert_element_type x1 -> x0, other arithmetic: 4.35 us -> none  [shards(): new_master.astype(jnp.bfloat16)]
    reduce_max x3 -> x0, other arithmetic: 3.56 us -> none  [the longest x2 3.45 us: adam_step(): first_top = jnp.max(jnp.abs(first_new), axis=(1, 3)) + 1e-06]
  transfers between devices with their start and end apart: 2 -> 0, of which waited for: 2 -> 0; matrix products, arithmetic and copies ran while one was open for 0% -> 0% of each run, Pallas kernels for 0% -> 0%
where the time goes in v1:
time: 147 us
  Pallas kernels  131 us (89%)
  local copies, waits for them, and re-layouts  15.2 us (10%)
    pallas_call x1, Pallas kernels, shards(): pl.pallas_call(functools.partial(kernel, n, m, limit), out_shape=(jax.Sha...  131 us
    unnamed x14, local copies, waits for them, and re-layouts  15.2 us

profile of v1, /device:TPU:0, one launch (start us, length us, event | category | flops | bytes accessed | tf_op | source)
XLA Modules:
  0.0 146.6 jit_solution(16649182029388749729)
XLA Ops:
  0.6 1.4 copy.13.fscale_ref
  2.1 1.4 copy.14.sscale_ref
  3.5 130.7 %step.1 = (bf16[8,576,512]{2,1,0:T(8,128)(2,1)}, f32[576,512]{1,0:T(8,128)}, f32[576,512]{1,0:T(8,128)}, f32[576,512]{1,0:T(8,128)}, f32[144,1]{1,0:T(8,128)}, /*index=5*/f32[144,1]{1,0:T(8,128)}) custom-call(bf16[768,4608]{1,0:T(8,128)(2,1)} %x_hbm.1, bf16[768,512]{1,0:T(8,128)(2,1)} %cot_hbm.1, f32[576,512]{1,0:T(8,128)} %master_hbm.1, s32[576,512]{1,0:T(8,128)} %fc_hbm.1, ...), custom_call_target="tpu_custom_call" | custom-call | tf_op jit(solution)/shard_map/step/pallas_call | solution.py:487
  134.2 1.5 %copy.15 = f32[144,1]{0,1:T(1,128)} copy(f32[144,1]{1,0:T(8,128)} %get-tuple-element.22) | data formatting | bytes 1152
  135.7 1.5 %copy.16 = f32[144,1]{0,1:T(1,128)} copy(f32[144,1]{1,0:T(8,128)} %get-tuple-element.23) | data formatting | bytes 1152
  137.2 0.0 copy-start.2
  137.2 4.9 %copy.21 = bf16[4608,512]{1,0:T(8,128)(2,1)} copy(bf16[4608,512]{1,0:T(8,128)(2,1)} %bitcast.1) | data formatting | bytes 9437184
  142.1 0.0 copy-done.2
  142.1 0.0 copy-start.1
  142.1 1.0 copy.22
  143.2 0.7 copy-done.1
  143.8 0.0 copy-start
  143.8 1.0 copy.23
  144.9 0.7 copy-done
  145.5 1.0 copy.24
Async XLA Ops:
  137.2 4.9 %copy-start.2 = (f32[576,512]{1,0:T(8,128)S(1)}, f32[576,512]{1,0:T(8,128)}, u32[]{:S(2)}) copy-start(f32[576,512]{1,0:T(8,128)} %get-tuple-element.31) | copy-start | bytes 3538948
  142.1 1.7 %copy-start.1 = (f32[576,512]{1,0:T(8,128)S(1)}, f32[576,512]{1,0:T(8,128)}, u32[]{:S(2)}) copy-start(f32[576,512]{1,0:T(8,128)} %get-tuple-element.32) | copy-start | bytes 3538948
  143.8 1.7 %copy-start = (f32[576,512]{1,0:T(8,128)S(1)}, f32[576,512]{1,0:T(8,128)}, u32[]{:S(2)}) copy-start(f32[576,512]{1,0:T(8,128)} %get-tuple-element.33) | copy-start | bytes 3538948

commit v2 on v1

--- a/solution.py
+++ b/solution.py
@@ -50,6 +50,12 @@
     zs_s,
     zr,
     zr_s,
+    zts,
+    zts_s,
+    ztr,
+    ztr_s,
+    xt,
+    xt_s,
     master,
     fc,
     sc,
@@ -75,6 +81,9 @@
     zs_recv,
     zss_send,
     zss_recv,
+    zt_send,
+    zt_recv,
+    xt_sem,
     nd_send,
     nd_recv,
     nmx_send,
@@ -83,6 +92,9 @@
     wx_recv,
     wz_send,
     wz_recv,
+    wxt_sem,
+    wt_send,
+    wt_recv,
     wout_sem,
     out_sem,
 ):
@@ -92,6 +104,9 @@
     cols_total = x_v.shape[1]
     R = 96 if rows % 96 == 0 else rows
     NR = rows // R
+    NT = 1 if NR >= 6 else 0
+    NM = NR - NT
+    tail = NM
     Q = rows // QROWS
     REP = width // LANES
 
@@ -167,56 +182,76 @@
     def fold(v):
         return v.reshape(R // 8, 8, width)
 
-    def encode(block, dst, dst_s, top):
-        top = jnp.maximum(top, 1e-30)
+    def encode(block, r, dst, dst_s):
+        v = fold(part[at_rows(block, r), :])
+        top = jnp.maximum(jnp.max(jnp.abs(v), axis=0), 1e-30)
         dst_s[...] = top * (1.0 / CODE_MAX)
-        inv = (CODE_MAX / top)[None]
-
-        @pl.loop(0, NR)
-        def _(r):
-            v = jnp.round(fold(part[at_rows(block, r), :]) * inv).reshape(R, width)
-            dst[chunk_rows(r), :] = v.astype(jnp.int32).astype(jnp.int16)
-
-    def top_of(block):
-        def body(r, t):
-            return jnp.maximum(t, jnp.max(jnp.abs(fold(part[at_rows(block, r), :])), axis=0))
-
-        return lax.fori_loop(0, NR, body, jnp.zeros((8, width), jnp.float32))
-
-    def add(block, src, src_s):
-        s = src_s[...][None]
-
-        @pl.loop(0, NR)
-        def _(r):
-            v = fold(src[chunk_rows(r), :].astype(jnp.int32).astype(jnp.float32)) * s
-            part[at_rows(block, r), :] = part[at_rows(block, r), :] + v.reshape(R, width)
-
-    def pair_copies(c):
-        to = {"dp": mate}
+        v = jnp.round(v * (CODE_MAX / top)[None]).reshape(R, width)
+        dst[...] = v.astype(jnp.int32).astype(jnp.int16)
+
+    def decode(src, src_s):
+        return fold(src[...].astype(jnp.int32).astype(jnp.float32)) * src_s[...][None]
+
+    def add(block, r, src, src_s):
+        at = at_rows(block, r)
+        part[at, :] = part[at, :] + decode(src, src_s).reshape(R, width)
+
+    def remote(src, dst, send, recv, **to):
+        return pltpu.make_async_remote_copy(src, dst, send, recv, device_id=to, device_id_type=MESH)
+
+    def pair_copies(c, r):
+        k = c * NM + r
         return (
-            pltpu.make_async_remote_copy(
-                xs.at[c], xr.at[c], xs_send.at[c], xs_recv.at[c], device_id=to, device_id_type=MESH
-            ),
-            pltpu.make_async_remote_copy(
-                xs_s.at[c], xr_s.at[c], xss_send.at[c], xss_recv.at[c], device_id=to, device_id_type=MESH
-            ),
+            remote(xs.at[k], xr.at[k], xs_send.at[k], xs_recv.at[k], dp=mate),
+            remote(xs_s.at[k], xr_s.at[k], xss_send.at[k], xss_recv.at[k], dp=mate),
         )
 
-    def line_copies(c, slot, to):
-        to = {"dp": to}
+    def line_copies(c, r, way, to):
+        k = c * NM + r
+        t = (way * A + c) * NM + r
         return (
-            pltpu.make_async_remote_copy(
-                zs.at[c], zr.at[slot], zs_send.at[c], zs_recv.at[slot], device_id=to, device_id_type=MESH
-            ),
-            pltpu.make_async_remote_copy(
-                zs_s.at[c], zr_s.at[slot], zss_send.at[c], zss_recv.at[slot], device_id=to, device_id_type=MESH
-            ),
+            remote(zs.at[k], zr.at[t], zs_send.at[k], zs_recv.at[t], dp=to),
+            remote(zs_s.at[k], zr_s.at[t], zss_send.at[k], zss_recv.at[t], dp=to),
         )
+
+    def tail_copies(c, half, way, to):
+        k = c * B + half
+        t = (way * A + c) * B + half
+        return (
+            remote(zts.at[k], ztr.at[t], zt_send.at[0, k], zt_recv.at[0, t], dp=to),
+            remote(zts_s.at[k], ztr_s.at[t], zt_send.at[1, k], zt_recv.at[1, t], dp=to),
+        )
+
+    pair_tail = (
+        remote(xt.at[0], xt.at[1], xt_sem.at[0], xt_sem.at[1], dp=mate),
+        remote(xt_s.at[0], xt_s.at[1], xt_sem.at[2], xt_sem.at[3], dp=mate),
+    )
 
     cot_copy.wait()
     if not per_chunk:
         in_copy(0).wait()
         multiply(0, cols_total // 384)
+
+    def send_tail(c):
+        for way, on, to in ((0, c > a, me + B), (1, c < a, me - B)):
+
+            @pl.when(on)
+            def _():
+                for half in range(B):
+                    k = c * B + half
+                    encode(k, tail, zts.at[k], zts_s.at[k])
+                    for cp in tail_copies(c, half, way, to):
+                        cp.start()
+
+    def receive_tail(c, way):
+        for half in range(B):
+            t = (way * A + c) * B + half
+            for cp in tail_copies(c, half, way, me):
+                cp.wait_recv()
+            add(c * B + half, tail, ztr.at[t], ztr_s.at[t])
+
+    def starts(c):
+        return ((c > a) & (a == 0)) | ((c < a) & (a == A - 1))
 
     @pl.loop(0, A)
     def _(i):
@@ -225,48 +260,79 @@
             in_copy(c).wait()
             multiply(c * csize, csize // 384)
         block = c * B + (1 - b)
-        encode(block, xs.at[c], xs_s.at[c], top_of(block))
 
         @pl.when(i == 0)
         def _():
             pl.semaphore_wait(barrier, n - 1 + m - 1)
 
-        for cp in pair_copies(c):
-            cp.start()
-
-    def receive(c, slot):
-        for cp in line_copies(c, slot, me):
+        @pl.loop(0, NM)
+        def _(r):
+            k = c * NM + r
+            encode(block, r, xs.at[k], xs_s.at[k])
+            for cp in pair_copies(c, r):
+                cp.start()
+
+        if NT:
+
+            @pl.when(starts(c))
+            def _():
+                send_tail(c)
+
+    def receive(c, r, way):
+        t = (way * A + c) * NM + r
+        for cp in line_copies(c, r, way, me):
             cp.wait_recv()
-        add(c * B + b, zr.at[slot], zr_s.at[slot])
-
-    def forward(c, slot, to):
-        block = c * B + b
-        encode(block, zs.at[c], zs_s.at[c], top_of(block))
-        for cp in line_copies(c, slot, to):
+        add(c * B + b, r, zr.at[t], zr_s.at[t])
+
+    def forward(c, r, way, to):
+        k = c * NM + r
+        encode(c * B + b, r, zs.at[k], zs_s.at[k])
+        for cp in line_copies(c, r, way, to):
             cp.start()
 
     @pl.loop(0, A)
     def _(i):
         c = order(i)
-        for cp in pair_copies(c):
+        if NT:
+            for way, on in ((0, (c >= a) & (a > 0)), (1, (c <= a) & (a < A - 1))):
+
+                @pl.when(on)
+                def _():
+                    receive_tail(c, way)
+
+            @pl.when((c != a) & jnp.logical_not(starts(c)))
+            def _():
+                send_tail(c)
+
+            @pl.when(c == a)
+            def _():
+                encode(mate, tail, xt.at[0], xt_s.at[0])
+                for cp in pair_tail:
+                    cp.start()
+
+        @pl.loop(0, NM)
+        def _(r):
+            k = c * NM + r
+            for cp in pair_copies(c, r):
+                cp.wait_recv()
+            add(c * B + b, r, xr.at[k], xr_s.at[k])
+
+            for way, on in ((0, (c >= a) & (a > 0)), (1, (c <= a) & (a < A - 1))):
+
+                @pl.when(on)
+                def _():
+                    receive(c, r, way)
+
+            for way, on, to in ((0, c > a, me + B), (1, c < a, me - B)):
+
+                @pl.when(on)
+                def _():
+                    forward(c, r, way, to)
+
+    if NT:
+        for cp in pair_tail:
             cp.wait_recv()
-        add(c * B + b, xr.at[c], xr_s.at[c])
-
-        @pl.when((c >= a) & (a > 0))
-        def _():
-            receive(c, c)
-
-        @pl.when((c <= a) & (a < A - 1))
-        def _():
-            receive(c, A + c)
-
-        @pl.when(c > a)
-        def _():
-            forward(c, c, me + B)
-
-        @pl.when(c < a)
-        def _():
-            forward(c, A + c, me - B)
+        add(me, tail, xt.at[1], xt_s.at[1])
 
     def square(r, t):
         g = fold(part[at_rows(me, r), :])
@@ -312,16 +378,59 @@
 
     for cp in par_copies:
         cp.wait()
+    pick = lax.broadcasted_iota(jnp.int32, (Q, Q), 0) == lax.broadcasted_iota(jnp.int32, (Q, Q), 1)
+
+    def column(row):
+        return jnp.sum(jnp.where(pick, row, 0.0), axis=1, keepdims=True)
+
     for j in range(QROWS):
         every = pl.ds(j, Q, stride=QROWS)
-        row1[every, :] = jnp.broadcast_to(fscale_ref[...] * (1.0 / 127.0), (Q, LANES))
-        row2[every, :] = jnp.broadcast_to(sscale_ref[...] * (1.0 / 255.0), (Q, LANES))
+        row1[every, :] = jnp.broadcast_to(column(fscale_ref[...] * (1.0 / 127.0)), (Q, LANES))
+        row2[every, :] = jnp.broadcast_to(column(sscale_ref[...] * (1.0 / 255.0)), (Q, LANES))
 
     def wide(v):
         return jnp.concatenate([v] * REP, axis=1)
 
+    def piece(block, r):
+        return wbuf.at[block, chunk_rows(r), :]
+
+    def pair_weight(c, r, block):
+        k = c * NM + r
+        return remote(piece(block, r), piece(block, r), wx_send.at[k], wx_recv.at[k], dp=mate)
+
+    def line_weight(c, r, way, to):
+        k = c * NM + r
+        w = piece(c * B + b, r)
+        return remote(w, w, wz_send.at[way * A * NM + k], wz_recv.at[k], dp=to)
+
+    def pair_weight_tail(block):
+        return remote(piece(block, tail), piece(block, tail), wxt_sem.at[0], wxt_sem.at[1], dp=mate)
+
+    def line_weight_tail(c, half, way, to):
+        k = c * B + half
+        return remote(piece(k, tail), piece(k, tail), wt_send.at[way * n + k], wt_recv.at[k], dp=to)
+
+    def weight_out(block):
+        at = pl.ds(0, NM * R)
+        return pltpu.make_async_copy(wbuf.at[block, at, :], w_hbm.at[block, at, :], wout_sem.at[0, block])
+
+    def weight_tail_out(block):
+        return pltpu.make_async_copy(piece(block, tail), w_hbm.at[block, chunk_rows(tail), :], wout_sem.at[1, block])
+
+    def send_own(r):
+        @pl.when(a < A - 1)
+        def _():
+            line_weight(a, r, 0, me + B).start()
+
+        @pl.when(a > 0)
+        def _():
+            line_weight(a, r, 1, me - B).start()
+
+        pair_weight(a, r, me).start()
+
     @pl.loop(0, NR)
-    def _(r):
+    def _(k):
+        r = (k + NM) % NR
         at = chunk_rows(r)
         clipped = part[at_rows(me, r), :] * factor
         first_new = beta_one * (fc[at, :].astype(jnp.float32) * wide(row1[at, :])) + (1.0 - beta_one) * clipped
@@ -338,44 +447,23 @@
         nm_v[at, :] = new
         wbuf[me, at, :] = new.astype(jnp.bfloat16)
 
-    def pair_weight(c, block):
-        return pltpu.make_async_remote_copy(
-            wbuf.at[block],
-            wbuf.at[block],
-            wx_send.at[c],
-            wx_recv.at[c],
-            device_id={"dp": mate},
-            device_id_type=MESH,
-        )
-
-    def line_weight(c, way, to):
-        block = c * B + b
-        return pltpu.make_async_remote_copy(
-            wbuf.at[block],
-            wbuf.at[block],
-            wz_send.at[way * A + c],
-            wz_recv.at[c],
-            device_id={"dp": to},
-            device_id_type=MESH,
-        )
-
-    def weight_out(block):
-        return pltpu.make_async_copy(wbuf.at[block], w_hbm.at[block], wout_sem.at[block])
-
-    @pl.when(a < A - 1)
-    def _():
-        line_weight(a, 0, me + B).start()
-
-    @pl.when(a > 0)
-    def _():
-        line_weight(a, 1, me - B).start()
-
-    pair_weight(a, me).start()
-    weight_out(me).start()
+        if NT:
+
+            @pl.when(r == tail)
+            def _():
+                pair_weight_tail(me).start()
+
+        @pl.when(r < NM)
+        def _():
+            send_own(r)
+
     nm_out_copy = pltpu.make_async_copy(nm_v, nm_hbm, out_sem.at[0])
     fu_out_copy = pltpu.make_async_copy(fu_v, fu_hbm, out_sem.at[1])
     su_out_copy = pltpu.make_async_copy(su_v, su_hbm, out_sem.at[2])
     nm_out_copy.start()
+    weight_out(me).start()
+    if NT:
+        weight_tail_out(me).start()
 
     @pl.loop(0, NR)
     def _(r):
@@ -388,7 +476,7 @@
         for j in range(1, QROWS):
             top = jnp.maximum(top, row[pl.ds(j, Q, stride=QROWS), :])
         top = top + 1e-06
-        top_ref[...] = top[:, :1]
+        top_ref[...] = jnp.sum(jnp.where(pick, top[:, :1], 0.0), axis=0, keepdims=True)
         for j in range(QROWS):
             row[pl.ds(j, Q, stride=QROWS), :] = 1.0 / top
 
@@ -401,74 +489,132 @@
     fu_out_copy.start()
     su_out_copy.start()
 
+    sides = ((0, lambda d: a - d, me + B, a < A - 1), (1, lambda d: a + d, me - B, a > 0))
+
+    def inside(c):
+        return (c >= 0) & (c < A)
+
     @pl.loop(1, A)
     def _(d):
-        @pl.when(a - d >= 0)
-        def _():
-            c = a - d
-            line_weight(c, 0, me).wait_recv()
-
-            @pl.when(a < A - 1)
-            def _():
-                line_weight(c, 0, me + B).start()
-
-            pair_weight(c, c * B + b).start()
-            weight_out(c * B + b).start()
-
-        @pl.when(a + d < A)
-        def _():
-            c = a + d
-            line_weight(c, 1, me).wait_recv()
-
-            @pl.when(a > 0)
-            def _():
-                line_weight(c, 1, me - B).start()
-
-            pair_weight(c, c * B + b).start()
-            weight_out(c * B + b).start()
-
-        @pl.when(d == 1)
-        def _():
-            pair_weight(a, mate).wait_recv()
-            weight_out(mate).start()
+        @pl.loop(0, NM)
+        def _(r):
+            for way, chunk, to, on in sides:
+                c = chunk(d)
+
+                @pl.when(inside(c))
+                def _():
+                    line_weight(c, r, way, me).wait_recv()
+
+                    @pl.when(on)
+                    def _():
+                        line_weight(c, r, way, to).start()
+
+                    pair_weight(c, r, c * B + b).start()
+
+        for way, chunk, to, on in sides:
+            c = chunk(d)
+
+            @pl.when(inside(c))
+            def _():
+                weight_out(c * B + b).start()
+
+        if NT:
+
+            @pl.when(d == 1)
+            def _():
+                pair_weight_tail(mate).wait_recv()
+                weight_tail_out(mate).start()
+                for half in range(B):
+                    for way, chunk, to, on in sides:
+
+                        @pl.when(on)
+                        def _():
+                            line_weight_tail(a, half, way, to).start()
+
+    if NT:
+
+        @pl.loop(1, A)
+        def _(d):
+            for half in range(B):
+                for way, chunk, to, on in sides:
+                    c = chunk(d)
+
+                    @pl.when(inside(c))
+                    def _():
+                        line_weight_tail(c, half, way, me).wait_recv()
+
+                        @pl.when(on)
+                        def _():
+                            line_weight_tail(c, half, way, to).start()
+
+                        weight_tail_out(c * B + half).start()
+
+    def take_pair(c):
+        @pl.loop(0, NM)
+        def _(r):
+            pair_weight(c, r, c * B + 1 - b).wait_recv()
+
+        weight_out(c * B + 1 - b).start()
+
+    take_pair(a)
 
     @pl.loop(1, A)
     def _(d):
-        @pl.when(a - d >= 0)
-        def _():
-            c = a - d
-            pair_weight(c, c * B + 1 - b).wait_recv()
-            weight_out(c * B + 1 - b).start()
-
-        @pl.when(a + d < A)
-        def _():
-            c = a + d
-            pair_weight(c, c * B + 1 - b).wait_recv()
-            weight_out(c * B + 1 - b).start()
+        for way, chunk, to, on in sides:
+            c = chunk(d)
+
+            @pl.when(inside(c))
+            def _():
+                take_pair(c)
 
     @pl.loop(0, A)
     def _(c):
-        for cp in pair_copies(c):
+        @pl.loop(0, NM)
+        def _(r):
+            for cp in pair_copies(c, r):
+                cp.wait_send()
+
+            @pl.when(c != a)
+            def _():
+                for cp in line_copies(c, r, 0, me):
+                    cp.wait_send()
+
+            pair_weight(c, r, c * B + b).wait_send()
+
+            @pl.when((c <= a) & (a < A - 1))
+            def _():
+                line_weight(c, r, 0, me).wait_send()
+
+            @pl.when((c >= a) & (a > 0))
+            def _():
+                line_weight(c, r, 1, me).wait_send()
+
+        if NT:
+            for half in range(B):
+
+                @pl.when(c != a)
+                def _():
+                    for cp in tail_copies(c, half, 0, me):
+                        cp.wait_send()
+
+                @pl.when((c <= a) & (a < A - 1))
+                def _():
+                    line_weight_tail(c, half, 0, me).wait_send()
+
+                @pl.when((c >= a) & (a > 0))
+                def _():
+                    line_weight_tail(c, half, 1, me).wait_send()
+
+    if NT:
+        for cp in pair_tail:
             cp.wait_send()
-
-        @pl.when(c != a)
-        def _():
-            for cp in line_copies(c, c, me):
-                cp.wait_send()
-
-        pair_weight(c, c * B + b).wait_send()
-
-        @pl.when((c <= a) & (a < A - 1))
-        def _():
-            line_weight(c, 0, me).wait_send()
-
-        @pl.when((c >= a) & (a > 0))
-        def _():
-            line_weight(c, 1, me).wait_send()
+        pair_weight_tail(me).wait_send()
 
     @pl.loop(0, n)
     def _(k):
         weight_out(k).wait()
+        if NT:
+            weight_tail_out(k).wait()
 
     nm_out_copy.wait()
     fu_out_copy.wait()
@@ -479,6 +625,10 @@
     rows, width = master.shape
     tokens, cols = inputs.shape
     A = n // 2
+    R = 96 if rows % 96 == 0 else rows
+    NR = rows // R
+    NM = NR - 1 if NR >= 6 else NR
+    Q = rows // QROWS
     f32 = jnp.float32
     any_spec = pl.BlockSpec(memory_space=pl.ANY)
     vmem_spec = pl.BlockSpec(memory_space=pltpu.VMEM)
@@ -491,8 +641,8 @@
             jax.ShapeDtypeStruct(block, f32),
             jax.ShapeDtypeStruct(block, f32),
             jax.ShapeDtypeStruct(block, f32),
-            jax.ShapeDtypeStruct(first_scale.shape, f32),
-            jax.ShapeDtypeStruct(second_scale.shape, f32),
+            jax.ShapeDtypeStruct((1, Q), f32),
+            jax.ShapeDtypeStruct((1, Q), f32),
         ),
         in_specs=[any_spec] * 5 + [vmem_spec] * 2,
         out_specs=[any_spec] * 4 + [vmem_spec] * 2,
@@ -500,14 +650,20 @@
             pltpu.VMEM((tokens, cols), jnp.bfloat16),
             pltpu.VMEM(key_cotangent.shape, jnp.bfloat16),
             pltpu.VMEM((cols, width), f32),
-            pltpu.VMEM((A, rows, width), jnp.int16),
-            pltpu.VMEM((A, 8, width), f32),
-            pltpu.VMEM((A, rows, width), jnp.int16),
-            pltpu.VMEM((A, 8, width), f32),
-            pltpu.VMEM((A, rows, width), jnp.int16),
-            pltpu.VMEM((A, 8, width), f32),
-            pltpu.VMEM((2 * A, rows, width), jnp.int16),
-            pltpu.VMEM((2 * A, 8, width), f32),
+            pltpu.VMEM((A * NM, R, width), jnp.int16),
+            pltpu.VMEM((A * NM, 8, width), f32),
+            pltpu.VMEM((A * NM, R, width), jnp.int16),
+            pltpu.VMEM((A * NM, 8, width), f32),
+            pltpu.VMEM((A * NM, R, width), jnp.int16),
+            pltpu.VMEM((A * NM, 8, width), f32),
+            pltpu.VMEM((2 * A * NM, R, width), jnp.int16),
+            pltpu.VMEM((2 * A * NM, 8, width), f32),
+            pltpu.VMEM((n, R, width), jnp.int16),
+            pltpu.VMEM((n, 8, width), f32),
+            pltpu.VMEM((2 * n, R, width), jnp.int16),
+            pltpu.VMEM((2 * n, 8, width), f32),
+            pltpu.VMEM((2, R, width), jnp.int16),
+            pltpu.VMEM((2, 8, width), f32),
             pltpu.VMEM(block, f32),
             pltpu.VMEM(block, jnp.int32),
             pltpu.VMEM(block, jnp.int32),
@@ -525,32 +681,38 @@
             pltpu.VMEM((m, 8, LANES), f32),
             dma((A,)),
             dma((4,)),
-            dma((A,)),
-            dma((A,)),
-            dma((A,)),
-            dma((A,)),
-            dma((A,)),
-            dma((2 * A,)),
-            dma((A,)),
-            dma((2 * A,)),
+            dma((A * NM,)),
+            dma((A * NM,)),
+            dma((A * NM,)),
+            dma((A * NM,)),
+            dma((A * NM,)),
+            dma((2 * A * NM,)),
+            dma((A * NM,)),
+            dma((2 * A * NM,)),
+            dma((2, n)),
+            dma((2, 2 * n)),
+            dma((4,)),
             dma((n,)),
             dma((n,)),
             dma((m,)),
             dma((m,)),
-            dma((A,)),
-            dma((A,)),
-            dma((2 * A,)),
-            dma((A,)),
+            dma((A * NM,)),
+            dma((A * NM,)),
+            dma((2 * A * NM,)),
+            dma((A * NM,)),
+            dma((2,)),
+            dma((2 * n,)),
             dma((n,)),
+            dma((2, n)),
             dma((3,)),
         ],
         compiler_params=pltpu.CompilerParams(
             collective_id=0, has_side_effects=True, vmem_limit_bytes=62 * 1024 * 1024
         ),
         name="step",
-    )(inputs, key_cotangent, master, first_codes, second_codes, first_scale, second_scale)
+    )(inputs, key_cotangent, master, first_codes, second_codes, first_scale.reshape(1, Q), second_scale.reshape(1, Q))
     weight = outs[0].reshape(n * rows, width)
-    return (weight, *outs[1:])
+    return (weight, *outs[1:4], outs[4].reshape(Q, 1), outs[5].reshape(Q, 1))
 
 
 def solution(mesh):

time: 147 us -> 139 us (0.946)
  local copies, waits for them, and re-layouts: 15.2 us -> 10.5 us
  Pallas kernels: 131 us -> 128 us
    unnamed x14 -> x16, local copies, waits for them, and re-layouts: 15.2 us -> 10.5 us
    pallas_call x1, Pallas kernels: 131 us -> 128 us  [shards(): pl.pallas_call(functools.partial(kernel, n, m, limit), out_shape=(jax.Sha...]
where the time goes in v2:
time: 139 us
  Pallas kernels  128 us (92%)
  local copies, waits for them, and re-layouts  10.5 us (8%)
    pallas_call x1, Pallas kernels, shards(): pl.pallas_call(functools.partial(kernel, n, m, limit), out_shape=(jax.Sha...  128 us
    unnamed x16, local copies, waits for them, and re-layouts  10.5 us

profile of v2, /device:TPU:0, one launch (start us, length us, event | category | flops | bytes accessed | tf_op | source)
XLA Modules:
  0.0 138.7 jit_solution(997495548953446024)
XLA Ops:
  0.6 127.6 %step.1 = (bf16[8,576,512]{2,1,0:T(8,128)(2,1)}, f32[576,512]{1,0:T(8,128)}, f32[576,512]{1,0:T(8,128)}, f32[576,512]{1,0:T(8,128)}, f32[1,144]{1,0:T(1,128)}, /*index=5*/f32[1,144]{1,0:T(1,128)}) custom-call(bf16[768,4608]{1,0:T(8,128)(2,1)} %x_hbm.1, bf16[768,512]{1,0:T(8,128)(2,1)} %cot_hbm.1, f32[576,512]{1,0:T(8,128)} %master_hbm.1, s32[576,512]{1,0:T(8,128)} %fc_hbm.1, ...), custom_call_target="tpu_custom_call" | custom-call | tf_op jit(solution)/shard_map/step/pallas_call | solution.py:637
  128.2 0.0 copy-start.2
  128.3 4.9 %copy.19 = bf16[4608,512]{1,0:T(8,128)(2,1)} copy(bf16[4608,512]{1,0:T(8,128)(2,1)} %bitcast.5) | data formatting | bytes 9437184
  133.2 0.0 copy-done.2
  133.2 0.0 copy-start.1
  133.2 1.0 copy.20
  134.2 0.7 copy-done.1
  134.9 0.0 copy-start
  134.9 1.0 copy.21
  135.9 0.7 copy-done
  136.6 0.0 copy-start.4
  136.6 0.0 copy-start.3
  136.6 1.0 copy.22
  137.6 0.0 copy-done.4
  137.6 0.6 copy.23
  138.2 0.0 copy-done.3
  138.2 0.6 copy.24
Async XLA Ops:
  128.2 4.9 %copy-start.2 = (f32[576,512]{1,0:T(8,128)S(1)}, f32[576,512]{1,0:T(8,128)}, u32[]{:S(2)}) copy-start(f32[576,512]{1,0:T(8,128)} %get-tuple-element.25) | copy-start | bytes 3538948
  133.2 1.7 %copy-start.1 = (f32[576,512]{1,0:T(8,128)S(1)}, f32[576,512]{1,0:T(8,128)}, u32[]{:S(2)}) copy-start(f32[576,512]{1,0:T(8,128)} %get-tuple-element.26) | copy-start | bytes 3538948
  134.9 1.7 %copy-start = (f32[576,512]{1,0:T(8,128)S(1)}, f32[576,512]{1,0:T(8,128)}, u32[]{:S(2)}) copy-start(f32[576,512]{1,0:T(8,128)} %get-tuple-element.27) | copy-start | bytes 3538948
  136.6 1.0 copy-start.4
  136.6 1.6 %copy-start.3 = (f32[1,144]{1,0:T(1,128)S(1)}, f32[1,144]{1,0:T(1,128)}, u32[]{:S(2)}) copy-start(f32[1,144]{1,0:T(1,128)} %get-tuple-element.17) | copy-start | bytes 1732

commit v3 on v2

--- a/solution.py
+++ b/solution.py
@@ -145,15 +145,7 @@
         for k, (src, dst) in enumerate(((master_hbm, master), (fc_hbm, fc), (sc_hbm, sc)))
     ]
     cot_copy.start()
-    if per_chunk:
-
-        @pl.loop(0, A)
-        def _(i):
-            in_copy(order(i)).start()
-    else:
-        in_copy(0).start()
-    for cp in par_copies:
-        cp.start()
+    in_copy(order(0) if per_chunk else 0).start()
 
     barrier = pltpu.get_barrier_semaphore()
 
@@ -183,18 +175,19 @@
         return v.reshape(R // 8, 8, width)
 
     def encode(block, r, dst, dst_s):
-        v = fold(part[at_rows(block, r), :])
-        top = jnp.maximum(jnp.max(jnp.abs(v), axis=0), 1e-30)
+        v = part[at_rows(block, r), :]
+        top = jnp.max(jnp.max(jnp.abs(fold(v)), axis=0), axis=0, keepdims=True)
+        top = jnp.maximum(top, 1e-30)
         dst_s[...] = top * (1.0 / CODE_MAX)
-        v = jnp.round(v * (CODE_MAX / top)[None]).reshape(R, width)
+        v = jnp.round(v * (CODE_MAX / top))
         dst[...] = v.astype(jnp.int32).astype(jnp.int16)
 
     def decode(src, src_s):
-        return fold(src[...].astype(jnp.int32).astype(jnp.float32)) * src_s[...][None]
+        return src[...].astype(jnp.int32).astype(jnp.float32) * src_s[...]
 
     def add(block, r, src, src_s):
         at = at_rows(block, r)
-        part[at, :] = part[at, :] + decode(src, src_s).reshape(R, width)
+        part[at, :] = part[at, :] + decode(src, src_s)
 
     def remote(src, dst, send, recv, **to):
         return pltpu.make_async_remote_copy(src, dst, send, recv, device_id=to, device_id_type=MESH)
@@ -258,6 +251,11 @@
         c = order(i)
         if per_chunk:
             in_copy(c).wait()
+
+            @pl.when(i < A - 1)
+            def _():
+                in_copy(order(i + 1)).start()
+
             multiply(c * csize, csize // 384)
         block = c * B + (1 - b)
 
@@ -277,6 +275,9 @@
             @pl.when(starts(c))
             def _():
                 send_tail(c)
+
+    for cp in par_copies:
+        cp.start()
 
     def receive(c, r, way):
         t = (way * A + c) * NM + r
@@ -651,19 +652,19 @@
             pltpu.VMEM(key_cotangent.shape, jnp.bfloat16),
             pltpu.VMEM((cols, width), f32),
             pltpu.VMEM((A * NM, R, width), jnp.int16),
-            pltpu.VMEM((A * NM, 8, width), f32),
+            pltpu.VMEM((A * NM, 1, width), f32),
             pltpu.VMEM((A * NM, R, width), jnp.int16),
-            pltpu.VMEM((A * NM, 8, width), f32),
+            pltpu.VMEM((A * NM, 1, width), f32),
             pltpu.VMEM((A * NM, R, width), jnp.int16),
-            pltpu.VMEM((A * NM, 8, width), f32),
+            pltpu.VMEM((A * NM, 1, width), f32),
             pltpu.VMEM((2 * A * NM, R, width), jnp.int16),
-            pltpu.VMEM((2 * A * NM, 8, width), f32),
+            pltpu.VMEM((2 * A * NM, 1, width), f32),
             pltpu.VMEM((n, R, width), jnp.int16),
-            pltpu.VMEM((n, 8, width), f32),
+            pltpu.VMEM((n, 1, width), f32),
             pltpu.VMEM((2 * n, R, width), jnp.int16),
-            pltpu.VMEM((2 * n, 8, width), f32),
+            pltpu.VMEM((2 * n, 1, width), f32),
             pltpu.VMEM((2, R, width), jnp.int16),
-            pltpu.VMEM((2, 8, width), f32),
+            pltpu.VMEM((2, 1, width), f32),
             pltpu.VMEM(block, f32),
             pltpu.VMEM(block, jnp.int32),
             pltpu.VMEM(block, jnp.int32),

time: 139 us -> 132 us (0.950)
  Pallas kernels: 128 us -> 121 us
    pallas_call x1, Pallas kernels: 128 us -> 121 us  [shards(): pl.pallas_call(functools.partial(kernel, n, m, limit), out_shape=(jax.Sha...]
where the time goes in v3:
time: 132 us
  Pallas kernels  121 us (92%)
  local copies, waits for them, and re-layouts  10.5 us (8%)
    pallas_call x1, Pallas kernels, shards(): pl.pallas_call(functools.partial(kernel, n, m, limit), out_shape=(jax.Sha...  121 us
    unnamed x16, local copies, waits for them, and re-layouts  10.5 us

profile of v3, /device:TPU:0, one launch (start us, length us, event | category | flops | bytes accessed | tf_op | source)
XLA Modules:
  0.0 131.7 jit_solution(8676181921266731810)
XLA Ops:
  0.6 120.6 %step.1 = (bf16[8,576,512]{2,1,0:T(8,128)(2,1)}, f32[576,512]{1,0:T(8,128)}, f32[576,512]{1,0:T(8,128)}, f32[576,512]{1,0:T(8,128)}, f32[1,144]{1,0:T(1,128)}, /*index=5*/f32[1,144]{1,0:T(1,128)}) custom-call(bf16[768,4608]{1,0:T(8,128)(2,1)} %x_hbm.1, bf16[768,512]{1,0:T(8,128)(2,1)} %cot_hbm.1, f32[576,512]{1,0:T(8,128)} %master_hbm.1, s32[576,512]{1,0:T(8,128)} %fc_hbm.1, ...), custom_call_target="tpu_custom_call" | custom-call | tf_op jit(solution)/shard_map/step/pallas_call | solution.py:638
  121.3 0.0 copy-start.2
  121.3 4.9 %copy.19 = bf16[4608,512]{1,0:T(8,128)(2,1)} copy(bf16[4608,512]{1,0:T(8,128)(2,1)} %bitcast.5) | data formatting | bytes 9437184
  126.2 0.0 copy-done.2
  126.2 0.0 copy-start.1
  126.2 1.0 copy.20
  127.2 0.7 copy-done.1
  127.9 0.0 copy-start
  127.9 1.0 copy.21
  128.9 0.7 copy-done
  129.6 0.0 copy-start.4
  129.6 0.0 copy-start.3
  129.6 1.0 copy.22
  130.6 0.0 copy-done.4
  130.6 0.6 copy.23
  131.2 0.0 copy-done.3
  131.2 0.6 copy.24
Async XLA Ops:
  121.3 4.9 %copy-start.2 = (f32[576,512]{1,0:T(8,128)S(1)}, f32[576,512]{1,0:T(8,128)}, u32[]{:S(2)}) copy-start(f32[576,512]{1,0:T(8,128)} %get-tuple-element.25) | copy-start | bytes 3538948
  126.2 1.7 %copy-start.1 = (f32[576,512]{1,0:T(8,128)S(1)}, f32[576,512]{1,0:T(8,128)}, u32[]{:S(2)}) copy-start(f32[576,512]{1,0:T(8,128)} %get-tuple-element.26) | copy-start | bytes 3538948
  127.9 1.7 %copy-start = (f32[576,512]{1,0:T(8,128)S(1)}, f32[576,512]{1,0:T(8,128)}, u32[]{:S(2)}) copy-start(f32[576,512]{1,0:T(8,128)} %get-tuple-element.27) | copy-start | bytes 3538948
  129.6 1.0 copy-start.4
  129.6 1.6 %copy-start.3 = (f32[1,144]{1,0:T(1,128)S(1)}, f32[1,144]{1,0:T(1,128)}, u32[]{:S(2)}) copy-start(f32[1,144]{1,0:T(1,128)} %get-tuple-element.17) | copy-start | bytes 1732
